TPU v7x, 8 devices: a whole 2x2x1 slice. The times are simulated.
8 devices in a mesh: dp: 1 (over z), tp: 8 (over x, y, core).
Axes of the slice: x: 2, y: 2, z: 1, core: 2. Of those that a mesh axis runs over, the one named last changes fastest.
Arguments:
- x: bfloat16 [2048, 2560], P('dp')
- dy: bfloat16 [2048, 2560], P('dp')
- gate: bfloat16 [2048, 10240], P('dp', 'tp')
- up: bfloat16 [2048, 10240], P('dp', 'tp')
- w_gate: bfloat16 [2560, 10240], P(None, 'tp')
- w_up: bfloat16 [2560, 10240], P(None, 'tp')
- w_down: bfloat16 [10240, 2560], P('tp')
Outputs:
- output 1: bfloat16 [2048, 2560], P('dp')
- output 2: bfloat16 [2560, 10240], P('dp', 'tp')
- output 3: bfloat16 [2560, 10240], P('dp', 'tp')
- output 4: bfloat16 [10240, 2560], P(('dp', 'tp'))
All inputs are finite; a program needn't handle non-finite values.
Results may differ from a plain program's by a relative error of at most 0.012.
Values are sent between devices in bfloat16 or wider.
A program may use at most 2 GiB of HBM per device.

v0:
```python
import jax
import jax.numpy as jnp
from jax import lax
from jax.experimental import pallas as pl
from jax.experimental.pallas import tpu as pltpu
from jax.sharding import PartitionSpec as P

MESH = pl.DeviceIdType.MESH
BF16, F32 = jnp.bfloat16, jnp.float32
SQRT_2_OVER_PI = 0.7978845608028654
CUBIC = 0.044715

T, D, F = 2048, 2560, 1280
N = 8
R = T // N
S = R // 2
Q = R // 4
H = D // 2
NT = 256
SLOTS = 4
STAGES = ("pair", "a", "b", "c", "own", "fwd", "e1", "e2")

TICKS = {
    "a": (7, 11, 15, 17, 24, 28, 35, 40),
    "b": (10, 15, 18, 21, 28, 32, 39, 45),
    "c": (13, 20, 23, 25, 34, 37, 43, 49),
    "d": (19, 29, 37, 42, 47, 49, 52, 54),
}


def dot_nt(a, b):
    return lax.dot_general(a, b, (((1,), (1,)), ((), ())), preferred_element_type=F32)


def kernel(x, dy, gate, up, wg, wu, wd, dx, dwg, dwu, dwd, dg, du, ht, dyb, xt, acc, pair_in, a_in, b_in, pair_out, a_out, b_out, w_sem, in_sem, x_sem, send_sem, recv_sem, free_sem):
    me = lax.axis_index("tp")
    core = lax.rem(me, 2)
    px, py = me // 4, lax.rem(me // 2, 2)
    p = jnp.where(core == 0, px, py)
    s = jnp.where(core == 0, py, px)
    over_x = (1 - px) * 4 + py * 2 + core
    over_y = px * 4 + (1 - py) * 2 + core
    n1 = jnp.where(core == 0, over_x, over_y)
    n2 = jnp.where(core == 0, over_y, over_x)
    partner = px * 4 + py * 2 + (1 - core)

    mine = pl.ds(pl.multiple_of(core * H, H), H)

    def rows(j, start, size):
        return pl.ds(pl.multiple_of(j * R + start, Q), size)

    def remote(stage, j, src, dst, to):
        k = STAGES.index(stage)
        return pltpu.make_async_remote_copy(src, dst, send_sem.at[k, j], recv_sem.at[k, j], device_id={"tp": to}, device_id_type=MESH)

    def copy_of(stage, j):
        if stage == "pair":
            return remote(stage, j, pair_out.at[lax.rem(j, 2)], pair_in.at[lax.rem(j, 2)], partner)
        if stage == "a":
            return remote(stage, j, a_out.at[lax.rem(j, SLOTS)], a_in.at[lax.rem(j, SLOTS)], n1)
        if stage == "b":
            return remote(stage, j, b_out.at[lax.rem(j, SLOTS)], b_in.at[j], n2)
        if stage == "c":
            at = dx.at[rows(j, S * p + Q * s, Q), mine]
            return remote(stage, j, at, at, n2)
        if stage == "own":
            at = dx.at[rows(j, S * p + Q * s, Q), mine]
            return remote(stage, j, at, at, n1)
        if stage == "fwd":
            at = dx.at[rows(j, S * p + Q * (1 - s), Q), mine]
            return remote(stage, j, at, at, n1)
        at = dx.at[rows(j, S * p if stage == "e1" else S * (1 - p), S), mine]
        return remote(stage, j, at, at, partner)

    def reuse(stage, j, slots):
        @pl.when(j >= slots)
        def _():
            copy_of(stage, j - slots).wait_send()

    def take_a(j):
        copy_of("a", j).wait_recv()
        reuse("b", j, SLOTS)
        k = lax.rem(j, SLOTS)
        keep, leave = pl.ds(pl.multiple_of(Q * s, Q), Q), pl.ds(pl.multiple_of(Q * (1 - s), Q), Q)
        b_out[k] = (acc[k, leave, :] + a_in[k, leave, :].astype(F32)).astype(BF16)
        copy_of("b", j).start()
        acc[k, keep, :] = acc[k, keep, :] + a_in[k, keep, :].astype(F32)

        @pl.when(j + SLOTS < N)
        def _():
            pl.semaphore_signal(free_sem, inc=1, device_id={"tp": n1}, device_id_type=MESH)

    def take_b(j):
        copy_of("b", j).wait_recv()
        keep = pl.ds(pl.multiple_of(Q * s, Q), Q)
        dx[rows(j, S * p + Q * s, Q), mine] = (acc[lax.rem(j, SLOTS), keep, :] + b_in[j].astype(F32)).astype(BF16)
        copy_of("c", j).start()
        copy_of("own", j).start()

    def take_c(j):
        copy_of("c", j).wait_recv()
        copy_of("fwd", j).start()
        copy_of("e1", j).start()

    def take_d(j):
        copy_of("own", j).wait_recv()
        copy_of("fwd", j).wait_recv()
        copy_of("e2", j).start()

    def tick(t, first, last):
        for name, take in (("a", take_a), ("b", take_b), ("c", take_c), ("d", take_d)):
            due = [(j, at) for j, at in enumerate(TICKS[name]) if first <= at <= last]
            if due:
                hit = sum((t == at).astype(jnp.int32) for _, at in due)
                j = sum((t == at).astype(jnp.int32) * j for j, at in due)

                @pl.when(hit > 0)
                def _(take=take, j=j):
                    take(j)

    def local(src, dst, sem):
        return pltpu.make_async_copy(src, dst, sem)

    def inputs(i):
        at = pl.ds(pl.multiple_of(i * R, R), R)
        return (
            local(dy.at[at], dyb, in_sem.at[0]),
            local(gate.at[at], dg.at[at], in_sem.at[1]),
            local(up.at[at], du.at[at], in_sem.at[2]),
        )

    weights = [local(src, dst, w_sem.at[k]) for k, (src, dst) in enumerate(((wd, dwd), (wg, dwg), (wu, dwu)))]
    weights[0].start()
    for c in inputs(0):
        c.start()
    weights[1].start()
    weights[2].start()

    barrier = pltpu.get_barrier_semaphore()
    for other in (n1, n2, partner):
        pl.semaphore_signal(barrier, inc=1, device_id={"tp": other}, device_id_type=MESH)
    pl.semaphore_wait(barrier, 3)

    def hidden_part(i):
        at = pl.ds(pl.multiple_of(i * R, R), R)
        dyv = dyb[...]
        for n in range(F // NT):
            cols = pl.ds(n * NT, NT)
            d_hidden = dot_nt(dyv, dwd[cols, :])
            g, u = dg[at, cols].astype(F32), du[at, cols].astype(F32)
            g2 = g * g
            h = 0.5 + 0.5 * jnp.tanh(g * (SQRT_2_OVER_PI + (SQRT_2_OVER_PI * CUBIC) * g2))
            a = g * h
            slope = h + (g * (h - h * h)) * (2 * SQRT_2_OVER_PI + (6 * SQRT_2_OVER_PI * CUBIC) * g2)
            dg[at, cols] = ((d_hidden * u) * slope).astype(BF16)
            du[at, cols] = (d_hidden * a).astype(BF16)
            ht[cols, at] = (a * u).astype(BF16).T

    def term(j, n, col0):
        at = pl.ds(pl.multiple_of(j * R, R), R)
        w = pl.ds(pl.multiple_of(col0 + n * NT, NT), NT)
        d = jnp.concatenate([dg[at, :], du[at, :]], axis=1)
        return dot_nt(d, jnp.concatenate([dwg[w, :], dwu[w, :]], axis=1))

    def pair_part(j):
        reuse("pair", j, 2)
        slot = lax.rem(j, 2)
        for n in range(H // NT):
            pair_out[slot, :, pl.ds(n * NT, NT)] = term(j, n, (1 - core) * H).astype(BF16)
        copy_of("pair", j).start()

    def own_part(j):
        copy_of("pair", j).wait_recv()
        reuse("a", j, SLOTS)
        slot, k = lax.rem(j, 2), lax.rem(j, SLOTS)
        for n in range(H // NT):
            cols = pl.ds(n * NT, NT)
            acc_t = term(j, n, core * H)
            tmp = acc_t + pair_in[slot, :, cols].astype(F32)
            lo, hi = tmp[:S], tmp[S:]
            kept = jnp.where(p == 0, lo, hi)
            sent = jnp.where(p == 0, hi, lo)
            acc[k, :, cols] = kept
            a_out[k, :, cols] = sent.astype(BF16)

        @pl.when(j >= SLOTS)
        def _():
            pl.semaphore_wait(free_sem, 1)

        copy_of("a", j).start()

    def chunk(i, _):
        for c in inputs(i):
            c.wait()

        @pl.when(i == 0)
        def _():
            weights[0].wait()

        hidden_part(i)

        @pl.when(i + 1 < N)
        def _():
            for c in inputs(i + 1):
                c.start()

        tick(3 * i, 0, 3 * N - 1)

        @pl.when(i == 0)
        def _():
            weights[1].wait()
            weights[2].wait()

        @pl.when(i > 0)
        def _():
            own_part(i - 1)

        tick(3 * i + 1, 0, 3 * N - 1)
        pair_part(i)
        tick(3 * i + 2, 0, 3 * N - 1)
        return ()

    lax.fori_loop(0, N, chunk, ())

    def tile(src, n):
        slot = lax.rem(n, 2)
        return local(src.at[:, pl.ds(pl.multiple_of(n * NT, NT), NT)], xt.at[slot], x_sem.at[slot])

    TILES = D // NT
    tile(dy, 0).start()
    own_part(N - 1)
    t0 = 3 * N
    tick(jnp.int32(t0), t0, t0)
    t0 += 1

    def down(n, _):
        tile(dy, n).wait()

        @pl.when(n + 1 < TILES)
        def _():
            tile(dy, n + 1).start()

        @pl.when(n + 1 == TILES)
        def _():
            tile(x, jnp.int32(TILES - TILES)).start()

        cols = pl.ds(pl.multiple_of(n * NT, NT), NT)
        dwd[:, cols] = jnp.dot(ht[...], xt[lax.rem(n, 2)], preferred_element_type=F32).astype(BF16)
        tick(t0 + n, t0, t0 + TILES - 1)
        return ()

    lax.fori_loop(0, TILES, down, ())
    t1 = t0 + TILES

    def gate_up(n, _):
        tile(x, n).wait()

        @pl.when(n + 1 < TILES)
        def _():
            tile(x, n + 1).start()

        at = pl.ds(pl.multiple_of(n * NT, NT), NT)
        xv = xt[lax.rem(n, 2)].T
        dwg[at, :] = jnp.dot(xv, dg[...], preferred_element_type=F32).astype(BF16)
        tick(t1 + 2 * n, t1, t1 + 2 * TILES - 1)
        dwu[at, :] = jnp.dot(xv, du[...], preferred_element_type=F32).astype(BF16)
        tick(t1 + 2 * n + 1, t1, t1 + 2 * TILES - 1)
        return ()

    lax.fori_loop(0, TILES, gate_up, ())

    def finish(j, _):
        copy_of("e1", j).wait_recv()
        copy_of("e2", j).wait_recv()
        for stage in STAGES[3:]:
            copy_of(stage, j).wait_send()
        for stage, slots in (("pair", 2), ("a", SLOTS), ("b", SLOTS)):

            @pl.when(j >= N - slots)
            def _(stage=stage):
                copy_of(stage, j).wait_send()

        return ()

    lax.fori_loop(0, N, finish, ())


def store(*refs):
    n = (len(refs) - 1) // 2
    copies = [pltpu.make_async_copy(refs[k], refs[n + k], refs[-1].at[k]) for k in range(n)]
    for c in copies:
        c.start()
    for c in copies:
        c.wait()


def solution(mesh):
    def step(x, dy, gate, up, w_gate, w_up, w_down):
        hbm = pl.BlockSpec(memory_space=pltpu.HBM)
        vmem = pl.BlockSpec(memory_space=pltpu.VMEM)
        dma = pltpu.SemaphoreType.DMA
        held = pl.pallas_call(
            kernel,
            name="mlp_backward",
            in_specs=[hbm] * 7,
            out_specs=[vmem] * 4,
            out_shape=[pltpu.VMEM((T, D), BF16), pltpu.VMEM((D, F), BF16), pltpu.VMEM((D, F), BF16), pltpu.VMEM((F, D), BF16)],
            scratch_shapes=[
                pltpu.VMEM((T, F), BF16),
                pltpu.VMEM((T, F), BF16),
                pltpu.VMEM((F, T), BF16),
                pltpu.VMEM((R, D), BF16),
                pltpu.VMEM((2, T, NT), BF16),
                pltpu.VMEM((SLOTS, S, H), F32),
                pltpu.VMEM((2, R, H), BF16),
                pltpu.VMEM((SLOTS, S, H), BF16),
                pltpu.VMEM((N, Q, H), BF16),
                pltpu.VMEM((2, R, H), BF16),
                pltpu.VMEM((SLOTS, S, H), BF16),
                pltpu.VMEM((SLOTS, Q, H), BF16),
                dma((3,)),
                dma((3,)),
                dma((2,)),
                dma((len(STAGES), N)),
                dma((len(STAGES), N)),
                pltpu.SemaphoreType.REGULAR,
            ],
            compiler_params=pltpu.CompilerParams(collective_id=0, has_side_effects=True, vmem_limit_bytes=35 * 2**20),
            cost_estimate=pl.CostEstimate(flops=12 * T * D * F, bytes_accessed=80 * 2**20, transcendentals=T * F),
        )(x, dy, gate, up, w_gate, w_up, w_down)
        return pl.pallas_call(
            store,
            name="store",
            in_specs=[vmem] * 4,
            out_specs=[hbm] * 4,
            out_shape=[jax.ShapeDtypeStruct(h.shape, BF16) for h in held],
            scratch_shapes=[dma((4,))],
            compiler_params=pltpu.CompilerParams(vmem_limit_bytes=2**20),
        )(*held)

    tokens, columns, down = P("dp", None), P(None, "tp"), P("tp", None)
    return jax.shard_map(
        step,
        mesh=mesh,
        in_specs=(tokens, tokens, P("dp", "tp"), P("dp", "tp"), columns, columns, down),
        out_specs=(tokens, P("dp", "tp"), P("dp", "tp"), P(("dp", "tp"), None)),
        check_vma=False,
    )
```

profile of v0, /device:TPU:0, one launch (start us, length us, event | category | flops | bytes accessed | tf_op | source)
XLA Modules:
  0.0 128.4 jit_solution(15230219472510046975)
XLA Ops:
  0.6 117.5 %mlp_backward.1 = (bf16[2048,2560]{1,0:T(8,128)(2,1)S(1)}, bf16[2560,1280]{1,0:T(8,128)(2,1)S(1)}, bf16[2560,1280]{1,0:T(8,128)(2,1)S(1)}, bf16[1280,2560]{1,0:T(8,128)(2,1)S(1)}) custom-call(bf16[2048,2560]{1,0:T(8,128)(2,1)} %x.1, bf16[2048,2560]{1,0:T(8,128)(2,1)} %dy.1, bf16[2048,1280]{1,0:T(8,128)(2,1)} %gate.1, bf16[2048,1280]{1,0:T(8,128)(2,1)} %up.1, ...), custom_call_target="tpu_custom_call" | custom-call | flops 80530636800 | bytes 83886080 | tf_op jit(solution)/shard_map/mlp_backward/pallas_call | solution.py:302
  118.2 10.2 %store.1 = (bf16[2048,2560]{1,0:T(8,128)(2,1)}, bf16[2560,1280]{1,0:T(8,128)(2,1)}, bf16[2560,1280]{1,0:T(8,128)(2,1)}, bf16[1280,2560]{1,0:T(8,128)(2,1)}) custom-call(bf16[2048,2560]{1,0:T(8,128)(2,1)S(1)} %get-tuple-element.8.refs_0_, bf16[2560,1280]{1,0:T(8,128)(2,1)S(1)} %get-tuple-element.9.refs_1_, bf16[2560,1280]{1,0:T(8,128)(2,1)S(1)} %get-tuple-element.10.refs_2_, ...), custom_call_target="tpu_custom_call" | custom-call | tf_op jit(solution)/shard_map/store/pallas_call | solution.py:331
where the time goes:
time: 128 us
  Pallas kernels  128 us (100%)
    pallas_call x1, Pallas kernels, step(): pl.pallas_call(kernel, name='mlp_backward', in_specs=[hbm] * 7, out_specs...  118 us
    pallas_call x1, Pallas kernels, step(): pl.pallas_call(store, name='store', in_specs=[vmem] * 4, out_specs=[hbm]...  10.2 us

commit v1 on v0

--- a/solution.py
+++ b/solution.py
@@ -21,10 +21,10 @@
 STAGES = ("pair", "a", "b", "c", "own", "fwd", "e1", "e2")
 
 TICKS = {
-    "a": (7, 11, 15, 17, 24, 28, 35, 40),
-    "b": (10, 15, 18, 21, 28, 32, 39, 45),
-    "c": (13, 20, 23, 25, 34, 37, 43, 49),
-    "d": (19, 29, 37, 42, 47, 49, 52, 54),
+    "a": (0, 4, 11, 12, 18, 22, 28, 31),
+    "b": (3, 8, 15, 17, 23, 27, 31, 34),
+    "c": (6, 11, 20, 21, 29, 34, 35, 36),
+    "d": (11, 20, 31, 34, 36, 43, 46, 47),
 }
 
 
@@ -129,17 +129,18 @@
             local(up.at[at], du.at[at], in_sem.at[2]),
         )
 
-    weights = [local(src, dst, w_sem.at[k]) for k, (src, dst) in enumerate(((wd, dwd), (wg, dwg), (wu, dwu)))]
-    weights[0].start()
-    for c in inputs(0):
+    def half(k):
+        at = pl.ds(pl.multiple_of((1 - core if k == 0 else core) * H, H), H)
+        return local(wg.at[at], dwg.at[at], w_sem.at[2 * k]), local(wu.at[at], dwu.at[at], w_sem.at[2 * k + 1])
+
+    down_weight = local(wd, dwd, w_sem.at[4])
+    down_weight.start()
+    for c in (*inputs(0), *half(0), *half(1)):
         c.start()
-    weights[1].start()
-    weights[2].start()
 
     barrier = pltpu.get_barrier_semaphore()
     for other in (n1, n2, partner):
         pl.semaphore_signal(barrier, inc=1, device_id={"tp": other}, device_id_type=MESH)
-    pl.semaphore_wait(barrier, 3)
 
     def hidden_part(i):
         at = pl.ds(pl.multiple_of(i * R, R), R)
@@ -169,58 +170,76 @@
             pair_out[slot, :, pl.ds(n * NT, NT)] = term(j, n, (1 - core) * H).astype(BF16)
         copy_of("pair", j).start()
 
-    def own_part(j):
+    def own_ready(j):
         copy_of("pair", j).wait_recv()
         reuse("a", j, SLOTS)
+
+        @pl.when(j >= SLOTS)
+        def _():
+            pl.semaphore_wait(free_sem, 1)
+
+    def own_part(j):
         slot, k = lax.rem(j, 2), lax.rem(j, SLOTS)
         for n in range(H // NT):
             cols = pl.ds(n * NT, NT)
-            acc_t = term(j, n, core * H)
-            tmp = acc_t + pair_in[slot, :, cols].astype(F32)
-            lo, hi = tmp[:S], tmp[S:]
-            kept = jnp.where(p == 0, lo, hi)
-            sent = jnp.where(p == 0, hi, lo)
-            acc[k, :, cols] = kept
-            a_out[k, :, cols] = sent.astype(BF16)
-
-        @pl.when(j >= SLOTS)
-        def _():
-            pl.semaphore_wait(free_sem, 1)
-
+            total = term(j, n, core * H) + pair_in[slot, :, cols].astype(F32)
+            lo, hi = total[:S], total[S:]
+            acc[k, :, cols] = jnp.where(p == 0, lo, hi)
+            a_out[k, :, cols] = jnp.where(p == 0, hi, lo).astype(BF16)
         copy_of("a", j).start()
 
-    def chunk(i, _):
+    def wait_inputs(i):
         for c in inputs(i):
             c.wait()
 
-        @pl.when(i == 0)
-        def _():
-            weights[0].wait()
-
+    def next_inputs(i):
+        @pl.when(i < N)
+        def _():
+            for c in inputs(i):
+                c.start()
+
+    zero, one = jnp.int32(0), jnp.int32(1)
+
+    def part(f, j):
+        @pl.when(me >= 0)
+        def _():
+            f(j)
+
+    wait_inputs(zero)
+    down_weight.wait()
+    part(hidden_part, zero)
+    next_inputs(one)
+    for c in half(0):
+        c.wait()
+    pl.semaphore_wait(barrier, 3)
+    part(pair_part, zero)
+    for c in half(1):
+        c.wait()
+    own_ready(zero)
+    part(own_part, zero)
+    wait_inputs(one)
+    part(hidden_part, one)
+    next_inputs(one + 1)
+    part(pair_part, one)
+    LAST = 3 * N - 7
+
+    def chunk(i, _):
+        wait_inputs(i)
         hidden_part(i)
-
-        @pl.when(i + 1 < N)
-        def _():
-            for c in inputs(i + 1):
-                c.start()
-
-        tick(3 * i, 0, 3 * N - 1)
-
-        @pl.when(i == 0)
-        def _():
-            weights[1].wait()
-            weights[2].wait()
-
-        @pl.when(i > 0)
+        next_inputs(i + 1)
+        tick(3 * i - 6, 0, LAST)
+        own_ready(i - 1)
+
+        @pl.when(i > 1)
         def _():
             own_part(i - 1)
 
-        tick(3 * i + 1, 0, 3 * N - 1)
+        tick(3 * i - 5, 0, LAST)
         pair_part(i)
-        tick(3 * i + 2, 0, 3 * N - 1)
-        return ()
-
-    lax.fori_loop(0, N, chunk, ())
+        tick(3 * i - 4, 0, LAST)
+        return ()
+
+    lax.fori_loop(2, N, chunk, ())
 
     def tile(src, n):
         slot = lax.rem(n, 2)
@@ -228,8 +247,9 @@
 
     TILES = D // NT
     tile(dy, 0).start()
-    own_part(N - 1)
-    t0 = 3 * N
+    own_ready(jnp.int32(N - 1))
+    own_part(jnp.int32(N - 1))
+    t0 = LAST + 1
     tick(jnp.int32(t0), t0, t0)
     t0 += 1
 
@@ -242,7 +262,7 @@
 
         @pl.when(n + 1 == TILES)
         def _():
-            tile(x, jnp.int32(TILES - TILES)).start()
+            tile(x, zero).start()
 
         cols = pl.ds(pl.multiple_of(n * NT, NT), NT)
         dwd[:, cols] = jnp.dot(ht[...], xt[lax.rem(n, 2)], preferred_element_type=F32).astype(BF16)
@@ -252,22 +272,39 @@
     lax.fori_loop(0, TILES, down, ())
     t1 = t0 + TILES
 
+    def turn(n):
+        ht[pl.ds(pl.multiple_of(lax.rem(n, 2) * NT, NT), NT), :] = xt[lax.rem(n, 2)].T
+
+    tile(x, zero).wait()
+    tile(x, one).start()
+    turn(zero)
+
     def gate_up(n, _):
-        tile(x, n).wait()
-
         @pl.when(n + 1 < TILES)
         def _():
-            tile(x, n + 1).start()
+            tile(x, n + 1).wait()
+
+        @pl.when(n + 2 < TILES)
+        def _():
+            tile(x, n + 2).start()
 
         at = pl.ds(pl.multiple_of(n * NT, NT), NT)
-        xv = xt[lax.rem(n, 2)].T
+        xv = ht[pl.ds(pl.multiple_of(lax.rem(n, 2) * NT, NT), NT), :]
         dwg[at, :] = jnp.dot(xv, dg[...], preferred_element_type=F32).astype(BF16)
-        tick(t1 + 2 * n, t1, t1 + 2 * TILES - 1)
+        turn(n + 1)
         dwu[at, :] = jnp.dot(xv, du[...], preferred_element_type=F32).astype(BF16)
-        tick(t1 + 2 * n + 1, t1, t1 + 2 * TILES - 1)
+        tick(t1 + n, t1, t1 + TILES - 1)
         return ()
 
     lax.fori_loop(0, TILES, gate_up, ())
+
+    t2 = t1 + TILES
+
+    def drain(t, _):
+        tick(t, t2, 99)
+        return ()
+
+    lax.fori_loop(t2, max(TICKS["d"]) + 1, drain, ())
 
     def finish(j, _):
         copy_of("e1", j).wait_recv()
@@ -318,7 +355,7 @@
                 pltpu.VMEM((2, R, H), BF16),
                 pltpu.VMEM((SLOTS, S, H), BF16),
                 pltpu.VMEM((SLOTS, Q, H), BF16),
-                dma((3,)),
+                dma((5,)),
                 dma((3,)),
                 dma((2,)),
                 dma((len(STAGES), N)),

time: 128 us -> 123 us (0.961)
  Pallas kernels: 128 us -> 121 us
    pallas_call x1, Pallas kernels: 118 us -> 111 us  [step(): pl.pallas_call(kernel, name='mlp_backward', in_specs=[hbm] * 7, out_specs...]
where the time goes in v1:
time: 123 us; the launch traced here: 122 us
  Pallas kernels  121 us (98%)
    pallas_call x1, Pallas kernels, step(): pl.pallas_call(kernel, name='mlp_backward', in_specs=[hbm] * 7, out_specs...  111 us
    pallas_call x1, Pallas kernels, step(): pl.pallas_call(store, name='store', in_specs=[vmem] * 4, out_specs=[hbm]...  10.2 us

profile of v1, /device:TPU:0, one launch (start us, length us, event | category | flops | bytes accessed | tf_op | source)
XLA Modules:
  0.0 122.3 jit_solution(2690239667598227029)
XLA Ops:
  0.6 111.3 %mlp_backward.1 = (bf16[2048,2560]{1,0:T(8,128)(2,1)S(1)}, bf16[2560,1280]{1,0:T(8,128)(2,1)S(1)}, bf16[2560,1280]{1,0:T(8,128)(2,1)S(1)}, bf16[1280,2560]{1,0:T(8,128)(2,1)S(1)}) custom-call(bf16[2048,2560]{1,0:T(8,128)(2,1)} %x.1, bf16[2048,2560]{1,0:T(8,128)(2,1)} %dy.1, bf16[2048,1280]{1,0:T(8,128)(2,1)} %gate.1, bf16[2048,1280]{1,0:T(8,128)(2,1)} %up.1, ...), custom_call_target="tpu_custom_call" | custom-call | flops 80530636800 | bytes 83886080 | tf_op jit(solution)/shard_map/mlp_backward/pallas_call | solution.py:339
  111.9 10.2 %store.1 = (bf16[2048,2560]{1,0:T(8,128)(2,1)}, bf16[2560,1280]{1,0:T(8,128)(2,1)}, bf16[2560,1280]{1,0:T(8,128)(2,1)}, bf16[1280,2560]{1,0:T(8,128)(2,1)}) custom-call(bf16[2048,2560]{1,0:T(8,128)(2,1)S(1)} %get-tuple-element.8.refs_0_, bf16[2560,1280]{1,0:T(8,128)(2,1)S(1)} %get-tuple-element.9.refs_1_, bf16[2560,1280]{1,0:T(8,128)(2,1)S(1)} %get-tuple-element.10.refs_2_, ...), custom_call_target="tpu_custom_call" | custom-call | tf_op jit(solution)/shard_map/store/pallas_call | solution.py:368

commit v2 on v1

--- a/solution.py
+++ b/solution.py
@@ -17,6 +17,7 @@
 Q = R // 4
 H = D // 2
 NT = 256
+PIECES = 4
 SLOTS = 4
 STAGES = ("pair", "a", "b", "c", "own", "fwd", "e1", "e2")
 
@@ -324,7 +325,12 @@
 
 def store(*refs):
     n = (len(refs) - 1) // 2
-    copies = [pltpu.make_async_copy(refs[k], refs[n + k], refs[-1].at[k]) for k in range(n)]
+    copies = []
+    for part in range(PIECES):
+        for k in range(n):
+            size = refs[k].shape[0] // PIECES
+            at = pl.ds(part * size, size)
+            copies.append(pltpu.make_async_copy(refs[k].at[at], refs[n + k].at[at], refs[-1].at[k, part]))
     for c in copies:
         c.start()
     for c in copies:
@@ -371,7 +377,7 @@
             in_specs=[vmem] * 4,
             out_specs=[hbm] * 4,
             out_shape=[jax.ShapeDtypeStruct(h.shape, BF16) for h in held],
-            scratch_shapes=[dma((4,))],
+            scratch_shapes=[dma((4, PIECES))],
             compiler_params=pltpu.CompilerParams(vmem_limit_bytes=2**20),
         )(*held)
 

time: 123 us -> 122 us (level)
  no operation moved by 1% of the time
where the time goes in v2:
time: 122 us
  Pallas kernels  121 us (99%)
    pallas_call x1, Pallas kernels, step(): pl.pallas_call(kernel, name='mlp_backward', in_specs=[hbm] * 7, out_specs...  111 us
    pallas_call x1, Pallas kernels, step(): pl.pallas_call(store, name='store', in_specs=[vmem] * 4, out_specs=[hbm]...  10 us

profile of v2, /device:TPU:0, one launch (start us, length us, event | category | flops | bytes accessed | tf_op | source)
XLA Modules:
  0.0 122.1 jit_solution(17069266790201706084)
XLA Ops:
  0.6 111.3 %mlp_backward.1 = (bf16[2048,2560]{1,0:T(8,128)(2,1)S(1)}, bf16[2560,1280]{1,0:T(8,128)(2,1)S(1)}, bf16[2560,1280]{1,0:T(8,128)(2,1)S(1)}, bf16[1280,2560]{1,0:T(8,128)(2,1)S(1)}) custom-call(bf16[2048,2560]{1,0:T(8,128)(2,1)} %x.1, bf16[2048,2560]{1,0:T(8,128)(2,1)} %dy.1, bf16[2048,1280]{1,0:T(8,128)(2,1)} %gate.1, bf16[2048,1280]{1,0:T(8,128)(2,1)} %up.1, ...), custom_call_target="tpu_custom_call" | custom-call | flops 80530636800 | bytes 83886080 | tf_op jit(solution)/shard_map/mlp_backward/pallas_call | solution.py:345
  111.9 10.0 %store.1 = (bf16[2048,2560]{1,0:T(8,128)(2,1)}, bf16[2560,1280]{1,0:T(8,128)(2,1)}, bf16[2560,1280]{1,0:T(8,128)(2,1)}, bf16[1280,2560]{1,0:T(8,128)(2,1)}) custom-call(bf16[2048,2560]{1,0:T(8,128)(2,1)S(1)} %get-tuple-element.8.refs_0_, bf16[2560,1280]{1,0:T(8,128)(2,1)S(1)} %get-tuple-element.9.refs_1_, bf16[2560,1280]{1,0:T(8,128)(2,1)S(1)} %get-tuple-element.10.refs_2_, ...), custom_call_target="tpu_custom_call" | custom-call | tf_op jit(solution)/shard_map/store/pallas_call | solution.py:374
